TPU v7x, 32 devices: a whole 2x2x4 slice. The times are simulated.
32 devices in a mesh: grp: 2 (over x), seq: 16 (over z, y, core).
Axes of the slice: x: 2, y: 2, z: 4, core: 2. Of those that a mesh axis runs over, the one named last changes fastest.
Arguments:
- queries: bfloat16 [8, 16, 8192], P('grp', 'seq'), parts along dimension 0, may hold values from -100 to 100
- answer_keys: bfloat16 [8, 16, 1024], P('grp', 'seq'), parts along dimension 0, may hold values from -6 to 6
- answer_values: bfloat16 [8, 16, 1024], P('grp', 'seq'), parts along dimension 0, may hold values from -6 to 6
- cached_prefix_keys: bfloat16 [2048, 1024], P(('grp', 'seq')), parts along dimension 0, may hold values from -5 to 5
- cached_prefix_values: bfloat16 [2048, 1024], P(('grp', 'seq')), parts along dimension 0, may hold values from -6 to 6
- residual: bfloat16 [8, 16, 8192], P('grp', 'seq'), parts along dimension 0, may hold values from -0.4375 to 0.4375
- out_weight: bfloat16 [8192, 8192], P('seq'), may hold values from -0.0625 to 0.0625
- norm_gain: float32 [8192], replicated, may hold values from 0.5 to 1.5
- head_weight: bfloat16 [8192, 65536], P(None, 'seq'), may hold values from -0.5745243 to 0.5745243
- targets: int32 [8, 16], P('grp'), parts along dimension 0, may hold values from 0 to 65535
- score_mask: int32 [8, 16], P('grp'), parts along dimension 0, may hold values 0 or 1
- lengths: int32 [8], P('grp'), parts along dimension 0, may hold values from 1 to 16, 40 in all
Outputs:
- logprobs: float32 [8, 16], P('grp', 'seq'), parts along dimension 0
- scores: float32 [8], P('grp'), parts along dimension 0
There are 2 independent parts, one for each index of `grp`. A program takes and returns all parts, laid end to end along the dimension named above; an argument that names none is the same for every part. Nothing has to cross between parts.
All inputs are finite; a program needn't handle non-finite values.
Results may differ from a plain program's by a relative error of at most 0.0013.
Values may be sent and summed in bfloat16 or wider, within the bound.
A program may use at most 128 MiB of HBM per device.

v0:
```python
import functools

import jax
import jax.numpy as jnp
from jax import lax
from jax.experimental import pallas as pl
from jax.experimental.pallas import tpu as pltpu
from jax.sharding import PartitionSpec as P

D = 8192
QUERY_HEADS = 64
KEY_VALUE_HEADS = 8
HEAD_SIZE = 128
CHOICE_COUNT = 4


def partner(block, axis, distance):
    count = lax.axis_size(axis)
    route = []
    for low in range(count):
        high = low | 1 << distance
        if high != low and high < count:
            route += [(low, high), (high, low)]
    return lax.ppermute(block, axis, route)


def combined_all(x, axis, combine):
    everything = jax.tree.map(lambda part: lax.all_gather(part, axis), x)
    leading = jax.tree.map(lambda part: part[0], everything)

    def hop(k, so_far):
        return combine(so_far, jax.tree.map(lambda part: part[k], everything))

    return lax.fori_loop(1, lax.axis_size(axis), hop, leading)


def per_device(
    queries,
    answer_keys,
    answer_values,
    cached_prefix_keys,
    cached_prefix_values,
    residual,
    out_weight,
    norm_gain,
    head_weight,
    targets,
    score_mask,
    lengths,
):
    seq_count = lax.axis_size("seq")
    myself = lax.axis_index("seq")
    local_length = queries.shape[1]
    full_len = local_length * seq_count
    groups = max(1, seq_count // QUERY_HEADS)
    per_dev = QUERY_HEADS * groups // seq_count
    grouped_heads = QUERY_HEADS // per_dev
    per_group = CHOICE_COUNT // groups
    repeat_count = grouped_heads // KEY_VALUE_HEADS
    local_prefix = cached_prefix_keys.shape[0]
    query_items = queries.reshape(
        groups, per_group, local_length, grouped_heads, per_dev * HEAD_SIZE
    )
    query_items = query_items.transpose(3, 0, 1, 2, 4).reshape(
        seq_count, per_group, local_length, per_dev * HEAD_SIZE
    )

    def choice_entries(input_array):
        expanded_heads = jnp.repeat(
            input_array.reshape(CHOICE_COUNT, local_length, KEY_VALUE_HEADS, HEAD_SIZE),
            repeat_count,
            axis=2,
        )
        expanded_heads = expanded_heads.reshape(
            groups, per_group, local_length, grouped_heads, HEAD_SIZE
        ).transpose(3, 0, 1, 2, 4)
        return expanded_heads.reshape(seq_count, per_group, local_length, HEAD_SIZE)

    def prefix_items(input_array):
        expanded_heads = jnp.repeat(
            input_array.reshape(local_prefix, KEY_VALUE_HEADS, HEAD_SIZE), repeat_count, axis=1
        ).transpose(1, 0, 2)
        expanded_heads = jnp.broadcast_to(
            expanded_heads[:, None, None], (grouped_heads, groups, 1, local_prefix, HEAD_SIZE)
        )
        return expanded_heads.reshape(seq_count, 1, local_prefix, HEAD_SIZE)

    head_queries, head_keys, head_values, head_pkeys, head_pvalues = (
        lax.all_to_all(query_items, "seq", split_axis=0, concat_axis=2, tiled=True),
        lax.all_to_all(choice_entries(answer_keys), "seq", split_axis=0, concat_axis=2, tiled=True),
        lax.all_to_all(
            choice_entries(answer_values), "seq", split_axis=0, concat_axis=2, tiled=True
        ),
        lax.all_to_all(
            prefix_items(cached_prefix_keys), "seq", split_axis=0, concat_axis=2, tiled=True
        ),
        lax.all_to_all(
            prefix_items(cached_prefix_values), "seq", split_axis=0, concat_axis=2, tiled=True
        ),
    )
    scaling = HEAD_SIZE ** (-0.5)
    query_vector = head_queries[0].reshape(per_group, full_len, per_dev, HEAD_SIZE)
    prefix_scores = (
        jnp.einsum(
            "clhd,pd->chlp", query_vector, head_pkeys[0, 0], preferred_element_type=jnp.float32
        )
        * scaling
    )
    choice_scores = (
        jnp.einsum("clhd,csd->chls", query_vector, head_keys[0], preferred_element_type=jnp.float32)
        * scaling
    )
    causal = lax.broadcasted_iota(jnp.int32, (full_len, full_len), 0) >= lax.broadcasted_iota(
        jnp.int32, (full_len, full_len), 1
    )
    choice_scores = jnp.where(causal, choice_scores, -1e30)
    row_peak = jnp.maximum(prefix_scores.max(-1), choice_scores.max(-1))[..., None]
    prefix_exp = jnp.exp(prefix_scores - row_peak)
    choice_exp = jnp.exp(choice_scores - row_peak)
    normalizer = prefix_exp.sum(-1, keepdims=True) + choice_exp.sum(-1, keepdims=True)
    attended_output_rows = jnp.einsum(
        "chlp,pd->clhd",
        (prefix_exp / normalizer).astype(jnp.bfloat16),
        head_pvalues[0, 0],
        preferred_element_type=jnp.float32,
    )
    attended_output_rows = attended_output_rows + jnp.einsum(
        "chls,csd->clhd",
        (choice_exp / normalizer).astype(jnp.bfloat16),
        head_values[0],
        preferred_element_type=jnp.float32,
    )
    attended_output_rows = attended_output_rows.astype(jnp.bfloat16).reshape(
        per_group, full_len, per_dev * HEAD_SIZE
    )
    result_output_rows = out_weight
    if groups > 1:
        peer_device = partner(result_output_rows, "seq", 0)
        is_lower = myself % 2 == 0
        result_output_rows = jnp.where(
            is_lower,
            jnp.concatenate([result_output_rows, peer_device], 0),
            jnp.concatenate([peer_device, result_output_rows], 0),
        )
    partial_rows = jnp.einsum(
        "omp,pu->omu", attended_output_rows, result_output_rows, preferred_element_type=jnp.float32
    )
    received = lax.all_to_all(partial_rows[None], "seq", split_axis=2, concat_axis=0, tiled=True)
    summed = (
        received.reshape(grouped_heads, groups, per_group, local_length, D)
        .sum(0)
        .reshape(CHOICE_COUNT, local_length, D)
    )
    hidden = residual.astype(jnp.float32) + summed
    inv_rms = lax.rsqrt(jnp.mean(hidden * hidden, -1, keepdims=True) + 1e-05)
    normalized_hidden = (hidden * inv_rms * norm_gain).astype(jnp.bfloat16)
    logits = jnp.einsum(
        "cld,dv->clv",
        lax.all_gather(normalized_hidden, "seq", axis=1, tiled=True),
        head_weight,
        preferred_element_type=jnp.float32,
    )
    vocab_local = head_weight.shape[1]
    offsets = targets - myself * vocab_local
    vocab_col = lax.broadcasted_iota(jnp.int32, logits.shape, 2)
    target_logit = jnp.sum(jnp.where(vocab_col == offsets[..., None], logits, 0.0), -1)
    local_max = logits.max(-1)

    def fold_stats(earlier, later):
        prefix_peak_score, sum_early, hit_early = earlier
        max_late, sum_late, hit_late = later
        joined = jnp.maximum(prefix_peak_score, max_late)
        return (
            joined,
            sum_early * jnp.exp(prefix_peak_score - joined) + sum_late * jnp.exp(max_late - joined),
            hit_early + hit_late,
        )

    global_max, exp_total, target_sum = combined_all(
        (local_max, jnp.sum(jnp.exp(logits - local_max[..., None]), -1), target_logit),
        "seq",
        fold_stats,
    )
    logprobs = target_sum - global_max - jnp.log(exp_total)
    positions = lax.broadcasted_iota(jnp.int32, (CHOICE_COUNT, full_len), 1)
    usable = jnp.where((score_mask == 1) & (positions < lengths[:, None]), 1.0, 0.0)
    counted = jnp.maximum(jnp.sum(usable, -1), 1.0)
    scores = jnp.sum(logprobs * usable, -1) / counted
    return (lax.dynamic_slice_in_dim(logprobs, myself * local_length, local_length, 1), scores)

MESH = pl.DeviceIdType.MESH
SLOTS = 13
F32, BF16 = jnp.float32, jnp.bfloat16


def across(column):
    rows = column.shape[0]
    wide = jnp.broadcast_to(column, (rows, 128))
    if rows < 128:
        wide = jnp.concatenate([wide, jnp.zeros((128 - rows, 128), F32)], 0)
    return wide.T[:8]


def down(lanes, rows):
    return jnp.broadcast_to(lanes[:1], (128, 128)).T[:rows, :1]


def fused_kernel(
    n,
    queries_ref,
    residual_ref,
    ak_ref,
    av_ref,
    pk_ref,
    pv_ref,
    gain_ref,
    tgt_ref,
    mask_ref,
    lengths_ref,
    ow_ref,
    hw_ref,
    out_ref,
    scores_ref,
    wbuf,
    q_ref,
    res_ref,
    akv_ref,
    kbuf,
    vbuf,
    abuf,
    qbuf,
    rbuf,
    rows32,
    att,
    psend,
    precv,
    ysend,
    yrecv,
    sbuf,
    rsbuf,
    ssq,
    xbuf,
    acc,
    stat,
    w_sem,
    ow_sem,
    k_sem,
    v_sem,
    a_sem,
    kf_sem,
    vf_sem,
    af_sem,
    q_sem,
    r_sem,
    p_sem,
    y_sem,
    rs_sem,
    ssq_sem,
    x_sem,
    xf_sem,
    st_sem,
):
    half = n // 2
    me = lax.axis_index("seq")
    chip, par = lax.div(me, 2), lax.rem(me, 2)
    other = chip * 2 + (1 - par)
    width = ow_ref.shape[1] // n
    depth = hw_ref.shape[0] // n
    vocab = hw_ref.shape[1]
    per_msg = q_ref.shape[1]
    sub = width // 128
    rows = n * per_msg // sub
    per_slot = vocab // width
    choices = per_msg // sub
    line = half // 2
    place, side = lax.div(chip, 2), lax.rem(chip, 2)
    beside = 2 * (2 * place + 1 - side) + par

    def dev(k, parity):
        return 2 * k + parity

    def ahead(d):
        return lax.rem(chip + d, half)

    def behind(d):
        return lax.rem(chip + half - d, half)

    def remote(src, dst, sems, i, target):
        return pltpu.make_async_remote_copy(
            src_ref=src,
            dst_ref=dst,
            send_sem=sems.at[0, i],
            recv_sem=sems.at[1, i],
            device_id={"seq": target},
            device_id_type=MESH,
        )

    def toward(e):
        z = lax.rem(place + lax.div(e, 2), line)
        return 2 * z + lax.rem(side + lax.rem(e, 2), 2)

    def arrived_from(e):
        z = lax.rem(place + line - lax.div(e, 2), line)
        return 2 * z + lax.rem(side + lax.rem(e, 2), 2)

    def turn(i):
        return jnp.where(i < 2, i, jnp.where(i <= line, 2 * (i - 1), 2 * (i - line) + 1))

    def source(t):
        return dev(arrived_from(turn(lax.div(t, 2))), lax.rem(par + lax.rem(t, 2), 2))

    def head_copy(t):
        first = pl.multiple_of(source(t) * depth, depth)
        return pltpu.make_async_copy(
            hw_ref.at[pl.ds(first, depth), :], wbuf.at[lax.rem(t, SLOTS)], w_sem.at[t]
        )

    def proj_copy(i):
        return pltpu.make_async_copy(
            ow_ref.at[:, pl.ds(pl.multiple_of(i * vocab, vocab), vocab)],
            wbuf.at[SLOTS - 2 + i],
            ow_sem.at[i],
        )

    proj_copy(0).start()
    proj_copy(1).start()

    @pl.loop(0, SLOTS - 2)
    def _(t):
        head_copy(t).start()

    barrier = pltpu.get_barrier_semaphore()

    @pl.loop(1, n)
    def _(d):
        pl.semaphore_signal(
            barrier, inc=1, device_id={"seq": lax.rem(me + d, n)}, device_id_type=MESH
        )

    def staged(ref, msg):
        @pl.loop(0, n)
        def _(j):
            for c in range(choices):
                for h in range(sub):
                    lanes = pl.ds(pl.multiple_of(j * width + h * 128, 128), 128)
                    row = pl.ds(j * per_msg + c * sub + h, 1)
                    rows32[row, :] = ref[c, :, lanes].astype(F32)

        msg[...] = rows32[...].reshape(n, per_msg, 128).astype(BF16)

    rows32[...] = jnp.zeros_like(rows32)

    @pl.loop(0, half)
    def _(k):
        lanes = pl.ds(pl.multiple_of(k * 128, 128), 128)
        for c in range(choices):
            rows32[pl.ds(k * 32 + c, 1), :] = ak_ref[c, :, lanes].astype(F32)
            rows32[pl.ds(k * 32 + 16 + c, 1), :] = av_ref[c, :, lanes].astype(F32)

    akv_ref[...] = rows32[...].reshape(half, 32, 128).astype(BF16)
    staged(queries_ref, q_ref)
    staged(residual_ref, res_ref)

    pl.semaphore_wait(barrier, n - 1)

    def kv_sends(d):
        k = ahead(d)
        cols = pl.ds(pl.multiple_of(k * 128, 128), 128)
        to = dev(k, par)
        return (
            remote(pk_ref.at[:, cols], kbuf.at[me], k_sem, d, to),
            remote(pv_ref.at[:, cols], vbuf.at[me], v_sem, d, to),
            remote(akv_ref.at[k], abuf.at[me], a_sem, d, to),
        )

    def kv_forwards(d):
        s = dev(behind(d), par)
        return (
            remote(kbuf.at[s], kbuf.at[s], kf_sem, d, other),
            remote(vbuf.at[s], vbuf.at[s], vf_sem, d, other),
            remote(abuf.at[s], abuf.at[s], af_sem, d, other),
        )

    def kv_arrivals(d):
        s = dev(behind(d), par)
        return (
            remote(kbuf.at[s], kbuf.at[s], k_sem, d, other),
            remote(vbuf.at[s], vbuf.at[s], v_sem, d, other),
            remote(abuf.at[s], abuf.at[s], a_sem, d, other),
        )

    def kv_relayed(d):
        s = dev(behind(d), 1 - par)
        return (
            remote(kbuf.at[s], kbuf.at[s], kf_sem, d, other),
            remote(vbuf.at[s], vbuf.at[s], vf_sem, d, other),
            remote(abuf.at[s], abuf.at[s], af_sem, d, other),
        )

    def kv_own():
        cols = pl.ds(pl.multiple_of(chip * 128, 128), 128)
        return (
            remote(pk_ref.at[:, cols], kbuf.at[me], kf_sem, 0, other),
            remote(pv_ref.at[:, cols], vbuf.at[me], vf_sem, 0, other),
            remote(akv_ref.at[chip], abuf.at[me], af_sem, 0, other),
        )

    def q_send(d):
        to = lax.rem(me + d, n)
        return remote(q_ref.at[to], qbuf.at[me], q_sem, d, to)

    def q_arrival(d):
        s = lax.rem(me + n - d, n)
        return remote(qbuf.at[s], qbuf.at[s], q_sem, d, other)

    def r_send(d):
        to = lax.rem(me + d, n)
        return remote(res_ref.at[to], rbuf.at[me], r_sem, d, to)

    def r_arrival(d):
        s = lax.rem(me + n - d, n)
        return remote(rbuf.at[s], rbuf.at[s], r_sem, d, other)

    @pl.loop(1, half)
    def _(d):
        for copy in kv_sends(d):
            copy.start()

    for copy in kv_own():
        copy.start()

    @pl.loop(1, n)
    def _(d):
        q_send(d).start()

    @pl.loop(1, n)
    def _(d):
        r_send(d).start()

    own_cols = pl.ds(pl.multiple_of(chip * 128, 128), 128)
    kbuf[me] = pk_ref[:, own_cols]
    vbuf[me] = pv_ref[:, own_cols]
    abuf[me] = akv_ref[chip]
    qbuf[me] = q_ref[me]
    rbuf[me] = res_ref[me]

    @pl.loop(1, half)
    def _(d):
        for arrived, onward in zip(kv_arrivals(d), kv_forwards(d)):
            arrived.wait_recv()
            onward.start()

    @pl.loop(1, n)
    def _(d):
        q_arrival(d).wait_recv()

    @pl.loop(0, half)
    def _(d):
        for copy in kv_relayed(d):
            copy.wait_recv()

    count = n * per_msg
    keys = kbuf[...].reshape(-1, 128)
    values = vbuf[...].reshape(-1, 128)
    own_keys = abuf[:, :16].reshape(-1, 128)
    own_values = abuf[:, 16:].reshape(-1, 128)
    scaling = HEAD_SIZE ** (-0.5)
    block = 64
    nt = (((1,), (1,)), ((), ()))

    @pl.loop(0, count // block)
    def _(i):
        per = block // per_msg
        qs = qbuf[pl.ds(i * per, per)].reshape(block, 128)
        ps = lax.dot_general(qs, keys, nt, preferred_element_type=F32) * scaling
        cs = lax.dot_general(qs, own_keys, nt, preferred_element_type=F32) * scaling
        row = lax.broadcasted_iota(jnp.int32, cs.shape, 0) + i * block
        col = lax.broadcasted_iota(jnp.int32, cs.shape, 1)
        choice = (row % per_msg) // sub
        seen = (choice == col % 16) & (col // 16 <= row // per_msg)
        cs = jnp.where(seen, cs, -1e30)
        top = jnp.maximum(ps.max(-1, keepdims=True), cs.max(-1, keepdims=True))
        pe, ce = jnp.exp(ps - top), jnp.exp(cs - top)
        inverse = 1.0 / (pe.sum(-1, keepdims=True) + ce.sum(-1, keepdims=True))
        mixed = jnp.dot((pe * inverse).astype(BF16), values, preferred_element_type=F32)
        mixed += jnp.dot((ce * inverse).astype(BF16), own_values, preferred_element_type=F32)
        rows32[pl.ds(pl.multiple_of(i * block, block), block), :] = mixed

    def regroup():
        return jnp.concatenate(
            [
                jnp.concatenate(
                    [rows32[pl.ds(c * sub + h, n, stride=per_msg), :] for h in range(sub)],
                    axis=1,
                )
                for c in range(choices)
            ],
            axis=0,
        )

    att[...] = regroup().astype(BF16)

    proj_copy(0).wait()
    proj_copy(1).wait()

    def projected(j):
        slot = SLOTS - 2 + lax.div(j, per_slot)
        cols = pl.ds(pl.multiple_of(lax.rem(j, per_slot) * width, width), width)
        return jnp.dot(att[...], wbuf[slot, :, cols], preferred_element_type=F32)

    def p_send(d):
        return remote(psend.at[d], precv.at[d], p_sem, d, other)

    def y_send(d):
        return remote(ysend.at[d], yrecv.at[d], y_sem, d, beside)

    def rs_send(d):
        return remote(sbuf.at[d], rsbuf.at[d], rs_sem, d, dev(toward(2 * d), par))

    def give(e):
        psend[e] = projected(dev(toward(e), 1 - par))
        p_send(e).start()

    def chip_sum(e):
        mine = projected(dev(toward(e), par))
        p_send(e).wait_recv()
        return mine + precv[e]

    @pl.loop(1, line + 1)
    def _(d):
        give(2 * lax.rem(d, line) + 1)

    @pl.loop(1, line + 1)
    def _(d):
        give(2 * lax.rem(d, line))

    @pl.loop(1, line + 1)
    def _(i):
        d = lax.rem(i, line)
        ysend[d] = chip_sum(2 * d + 1).astype(BF16)
        y_send(d).start()

    @pl.loop(1, line)
    def _(d):
        mine = chip_sum(2 * d)
        y_send(d).wait_recv()
        sbuf[d] = (mine + yrecv[d].astype(F32)).astype(BF16)
        rs_send(d).start()

    mine = chip_sum(0)

    @pl.loop(SLOTS - 2, SLOTS)
    def _(t):
        head_copy(t).start()

    @pl.loop(1, n)
    def _(d):
        r_arrival(d).wait_recv()

    rows32[...] = rbuf[...].astype(F32).reshape(count, 128)
    y_send(0).wait_recv()
    total = regroup() + (mine + yrecv[0].astype(F32))
    for d in range(1, line):
        rs_send(d).wait_recv()
        total = total + rsbuf[d].astype(F32)

    def ssq_send(d):
        return remote(ssq.at[me], ssq.at[me], ssq_sem, d, lax.rem(me + d, n))

    def ssq_arrival(d):
        s = lax.rem(me + n - d, n)
        return remote(ssq.at[s], ssq.at[s], ssq_sem, d, other)

    ssq[me] = across(jnp.sum(total * total, -1, keepdims=True))

    @pl.loop(1, n)
    def _(d):
        ssq_send(d).start()

    @pl.loop(1, n)
    def _(d):
        ssq_arrival(d).wait_recv()

    squares = down(jnp.sum(ssq[...], 0), rows)
    inv_rms = lax.rsqrt(squares / (n * width) + 1e-05)
    gain = gain_ref[:, pl.ds(pl.multiple_of(me * width, width), width)]
    xbuf[me] = (total * inv_rms * gain).astype(BF16)

    def x_send(d):
        return remote(xbuf.at[me], xbuf.at[me], x_sem, 2 * d, dev(toward(2 * d), par))

    def x_aside(e):
        s = dev(arrived_from(e), par)
        return remote(xbuf.at[s], xbuf.at[s], x_sem, e + 1, beside)

    def x_arrival(e):
        s = dev(arrived_from(e), par)
        return remote(xbuf.at[s], xbuf.at[s], x_sem, e, other)

    def x_forward(e):
        s = dev(arrived_from(e), par)
        return remote(xbuf.at[s], xbuf.at[s], xf_sem, e, other)

    def x_relayed(e):
        s = dev(arrived_from(e), 1 - par)
        return remote(xbuf.at[s], xbuf.at[s], xf_sem, e, other)

    x_aside(0).start()

    @pl.loop(1, line)
    def _(d):
        x_send(d).start()

    x_forward(0).start()
    acc[...] = jnp.zeros_like(acc)
    tile = 1024 if vocab % 1024 == 0 else vocab

    def step(t):
        head_copy(t).wait()
        slot = lax.rem(t, SLOTS)
        x = xbuf[source(t)]
        for first in range(0, vocab, tile):
            acc[:, first : first + tile] += jnp.dot(
                x, wbuf[slot, :, first : first + tile], preferred_element_type=F32
            )

        @pl.when(t + SLOTS < n)
        def _():
            head_copy(t + SLOTS).start()

    @pl.loop(0, half)
    def _(i):
        e = turn(i)

        @pl.when(i > 0)
        def _():
            x_arrival(e).wait_recv()

            @pl.when(lax.rem(e, 2) == 0)
            def _():
                x_aside(e).start()

            x_forward(e).start()

        step(2 * i)
        x_relayed(e).wait_recv()
        step(2 * i + 1)

    logits = acc[...]
    peak = logits.max(-1, keepdims=True)
    total_exp = jnp.sum(jnp.exp(logits - peak), -1, keepdims=True)
    vocab_col = lax.broadcasted_iota(jnp.int32, logits.shape, 1) + me * vocab
    hit = jnp.sum(jnp.where(vocab_col == tgt_ref[...], logits, 0.0), -1, keepdims=True)
    lane = lax.broadcasted_iota(jnp.int32, (8, 128), 0)
    stat[me] = jnp.where(
        lane == 0, across(peak), jnp.where(lane == 1, across(total_exp), across(hit))
    )

    def st_send(d):
        return remote(stat.at[me], stat.at[me], st_sem, d, lax.rem(me + d, n))

    def st_arrival(d):
        s = lax.rem(me + n - d, n)
        return remote(stat.at[s], stat.at[s], st_sem, d, other)

    @pl.loop(1, n)
    def _(d):
        st_send(d).start()

    @pl.loop(1, n)
    def _(d):
        st_arrival(d).wait_recv()

    everything = stat[...]
    peaks, sums, hits = everything[:, 0:1], everything[:, 1:2], everything[:, 2:3]
    top = jnp.max(peaks, 0)
    whole = jnp.sum(sums * jnp.exp(peaks - top[None]), 0)
    logprob = jnp.sum(hits, 0) - top - jnp.log(whole)
    table = jnp.concatenate([logprob[:, c * n : (c + 1) * n] for c in range(choices)], 0)
    position = lax.broadcasted_iota(jnp.int32, table.shape, 1)
    choice = lax.broadcasted_iota(jnp.int32, table.shape, 0)
    out_ref[...] = jnp.sum(jnp.where(position == me, table, 0.0), -1, keepdims=True)
    length = jnp.zeros(table.shape, jnp.int32)
    for c in range(choices):
        length = jnp.where(choice == c, lengths_ref[c], length)
    usable = jnp.where((mask_ref[...] == 1) & (position < length), 1.0, 0.0)
    counted = jnp.maximum(jnp.sum(usable, -1, keepdims=True), 1.0)
    means = jnp.sum(table * usable, -1, keepdims=True) / counted
    for c in range(choices):
        scores_ref[c] = jnp.sum(means[c : c + 1])

    @pl.loop(1, half)
    def _(d):
        for copy in kv_sends(d) + kv_forwards(d):
            copy.wait_send()

    @pl.loop(1, line)
    def _(d):
        rs_send(d).wait_send()
        x_send(d).wait_send()

    @pl.loop(0, line)
    def _(d):
        y_send(d).wait_send()
        x_aside(2 * d).wait_send()

    for copy in kv_own():
        copy.wait_send()

    @pl.loop(0, half)
    def _(d):
        p_send(d).wait_send()
        x_forward(d).wait_send()

    @pl.loop(1, n)
    def _(d):
        q_send(d).wait_send()
        r_send(d).wait_send()
        ssq_send(d).wait_send()
        st_send(d).wait_send()


def fused(
    queries,
    answer_keys,
    answer_values,
    cached_prefix_keys,
    cached_prefix_values,
    residual,
    out_weight,
    norm_gain,
    head_weight,
    targets,
    score_mask,
    lengths,
):
    n = lax.axis_size("seq")
    half = n // 2
    width = D // n
    sub = width // HEAD_SIZE
    per_msg = CHOICE_COUNT * sub
    rows = CHOICE_COUNT * n
    local_prefix = cached_prefix_keys.shape[0]
    vocab = head_weight.shape[1]
    vmem, hbm = (
        pl.BlockSpec(memory_space=pltpu.VMEM),
        pl.BlockSpec(memory_space=pl.ANY),
    )
    sems = pltpu.SemaphoreType.DMA
    smem = pl.BlockSpec(memory_space=pltpu.SMEM)
    message = pltpu.VMEM((n, per_msg, HEAD_SIZE), BF16)
    logprobs, scores = pl.pallas_call(
        functools.partial(fused_kernel, n),
        out_shape=(
            jax.ShapeDtypeStruct((CHOICE_COUNT, 1), F32),
            jax.ShapeDtypeStruct((CHOICE_COUNT,), F32),
        ),
        in_specs=[vmem] * 9 + [smem] + [hbm] * 2,
        out_specs=(vmem, smem),
        scratch_shapes=[
            pltpu.VMEM((SLOTS, width, vocab), BF16),
            message,
            message,
            pltpu.VMEM((half, 32, HEAD_SIZE), BF16),
            pltpu.VMEM((n, local_prefix, HEAD_SIZE), BF16),
            pltpu.VMEM((n, local_prefix, HEAD_SIZE), BF16),
            pltpu.VMEM((n, 32, HEAD_SIZE), BF16),
            pltpu.VMEM((n, per_msg, HEAD_SIZE), BF16),
            pltpu.VMEM((n, per_msg, HEAD_SIZE), BF16),
            pltpu.VMEM((n * per_msg, HEAD_SIZE), F32),
            pltpu.VMEM((rows, width), BF16),
            pltpu.VMEM((half, rows, width), F32),
            pltpu.VMEM((half, rows, width), F32),
            pltpu.VMEM((half // 2, rows, width), BF16),
            pltpu.VMEM((half // 2, rows, width), BF16),
            pltpu.VMEM((half // 2, rows, width), BF16),
            pltpu.VMEM((half // 2, rows, width), BF16),
            pltpu.VMEM((n, 8, 128), F32),
            pltpu.VMEM((n, rows, width), BF16),
            pltpu.VMEM((rows, vocab), F32),
            pltpu.VMEM((n, 8, 128), F32),
            sems((n,)),
            sems((2,)),
        ]
        + [sems((2, half))] * 6
        + [sems((2, n))] * 2
        + [sems((2, half))]
        + [sems((2, half // 2))] * 2
        + [sems((2, n))]
        + [sems((2, half))] * 2
        + [sems((2, n))],
        compiler_params=pltpu.CompilerParams(
            collective_id=0, has_side_effects=True, vmem_limit_bytes=67043328
        ),
    )(
        queries,
        residual,
        answer_keys,
        answer_values,
        cached_prefix_keys,
        cached_prefix_values,
        norm_gain.reshape(1, D),
        targets.reshape(rows, 1),
        score_mask,
        lengths,
        out_weight,
        head_weight,
    )
    return logprobs, scores


def either(*arrays):
    queries, head_weight = arrays[0], arrays[8]
    n = lax.axis_size("seq")
    small = n == 2 * KEY_VALUE_HEADS and queries.shape[1] == 1
    if small and head_weight.shape[1] * 2 == D:
        return fused(*arrays)
    return per_device(*arrays)


def solution(mesh):
    placed = (
        P("grp", "seq", None),
        P("grp", "seq", None),
        P("grp", "seq", None),
        P(("grp", "seq"), None),
        P(("grp", "seq"), None),
        P("grp", "seq", None),
        P("seq", None),
        P(),
        P(None, "seq"),
        P("grp", None),
        P("grp", None),
        P("grp"),
    )
    return jax.shard_map(
        either,
        mesh=mesh,
        in_specs=placed,
        out_specs=(P("grp", "seq"), P("grp")),
        check_vma=False,
    )
```

profile of v0, /device:TPU:0, one launch (start us, length us, event | category | flops | bytes accessed | tf_op | source)
XLA Modules:
  0.0 74.9 jit_solution(10926649317346507527)
XLA Ops:
  0.6 1.3 %copy.16.ak_ref = bf16[4,1,1024]{2,1,0:T(2,128)(2,1)} copy(bf16[4,1,1024]{2,0,1:T(4,128)(2,1)} %param.13) | data formatting | bytes 16384 | tf_op args[1]
  1.9 1.3 %copy.17.av_ref = bf16[4,1,1024]{2,1,0:T(2,128)(2,1)} copy(bf16[4,1,1024]{2,0,1:T(4,128)(2,1)} %param.14) | data formatting | bytes 16384 | tf_op args[2]
  3.2 1.4 %reshape.12.tgt_ref = s32[64,1]{1,0:T(8,128)} reshape(s32[4,16]{1,0:T(4,128)} %param.21) | data formatting | bytes 512 | tf_op jit(solution)/shard_map/reshape | solution.py:803
  4.6 1.6 %copy.14.queries_ref = bf16[4,1,8192]{2,1,0:T(2,128)(2,1)} copy(bf16[4,1,8192]{2,0,1:T(4,128)(2,1)} %param.12) | data formatting | bytes 131072 | tf_op args[0]
  6.2 1.6 %copy.15.residual_ref = bf16[4,1,8192]{2,1,0:T(2,128)(2,1)} copy(bf16[4,1,8192]{2,0,1:T(4,128)(2,1)} %param.17) | data formatting | bytes 131072 | tf_op args[5]
  7.8 64.7 %shard_map.131 = (f32[4,1]{1,0:T(4,128)}, f32[4]{0:T(128)}) custom-call(bf16[4,1,8192]{2,1,0:T(2,128)(2,1)} %copy.14.queries_ref, bf16[4,1,8192]{2,1,0:T(2,128)(2,1)} %copy.15.residual_ref, bf16[4,1,1024]{2,1,0:T(2,128)(2,1)} %copy.16.ak_ref, bf16[4,1,1024]{2,1,0:T(2,128)(2,1)} %copy.17.av_ref, bf16[64,1024]{1,0:T(8,128)(2,1)} %pk_ref.1, ...), custom_call_target="tpu_custom_call" | custom-call | tf_op jit(solution)/shard_map/pallas_call | solution.py:752
  72.5 1.3 %copy.19 = f32[4,1]{0,1:T(1,128)} copy(f32[4,1]{1,0:T(4,128)} %get-tuple-element.2) | data formatting | bytes 32 | tf_op jit(solution)/shard_map/pallas_call | solution.py:752
  73.8 1.1 %copy.21 = f32[4]{0:T(128)} copy(f32[4]{0:T(128)} %get-tuple-element.7) | data formatting | bytes 32
where the time goes:
time: 75.3 us; the launch traced here: 74.9 us
  Pallas kernels  64.7 us (86%)
  local copies, waits for them, and re-layouts  9.56 us (13%)
    pallas_call x1, Pallas kernels, fused(): pl.pallas_call(functools.partial(fused_kernel, n), out_shape=(jax.ShapeDt...  64.7 us
    unnamed x5, local copies, waits for them, and re-layouts  6.92 us

commit v1 on v0

--- a/solution.py
+++ b/solution.py
@@ -220,7 +220,6 @@
     ow_ref,
     hw_ref,
     out_ref,
-    scores_ref,
     wbuf,
     q_ref,
     res_ref,
@@ -344,7 +343,7 @@
                 for h in range(sub):
                     lanes = pl.ds(pl.multiple_of(j * width + h * 128, 128), 128)
                     row = pl.ds(j * per_msg + c * sub + h, 1)
-                    rows32[row, :] = ref[c, :, lanes].astype(F32)
+                    rows32[row, :] = ref[:, lanes].astype(F32)[c : c + 1]
 
         msg[...] = rows32[...].reshape(n, per_msg, 128).astype(BF16)
 
@@ -354,8 +353,8 @@
     def _(k):
         lanes = pl.ds(pl.multiple_of(k * 128, 128), 128)
         for c in range(choices):
-            rows32[pl.ds(k * 32 + c, 1), :] = ak_ref[c, :, lanes].astype(F32)
-            rows32[pl.ds(k * 32 + 16 + c, 1), :] = av_ref[c, :, lanes].astype(F32)
+            rows32[pl.ds(k * 32 + c, 1), :] = ak_ref[:, lanes].astype(F32)[c : c + 1]
+            rows32[pl.ds(k * 32 + 16 + c, 1), :] = av_ref[:, lanes].astype(F32)[c : c + 1]
 
     akv_ref[...] = rows32[...].reshape(half, 32, 128).astype(BF16)
     staged(queries_ref, q_ref)
@@ -649,8 +648,16 @@
     logits = acc[...]
     peak = logits.max(-1, keepdims=True)
     total_exp = jnp.sum(jnp.exp(logits - peak), -1, keepdims=True)
+    ids = tgt_ref[...].astype(F32)
+    row = lax.broadcasted_iota(jnp.int32, (rows, n), 0)
+    slot = lax.broadcasted_iota(jnp.int32, (rows, n), 1)
+    wanted = jnp.zeros((rows, n), F32)
+    for c in range(choices):
+        mine_here = (row // n == c) & (row % n == slot)
+        wanted = jnp.where(mine_here, ids[c : c + 1], wanted)
+    wanted = jnp.sum(wanted, -1, keepdims=True).astype(jnp.int32)
     vocab_col = lax.broadcasted_iota(jnp.int32, logits.shape, 1) + me * vocab
-    hit = jnp.sum(jnp.where(vocab_col == tgt_ref[...], logits, 0.0), -1, keepdims=True)
+    hit = jnp.sum(jnp.where(vocab_col == wanted, logits, 0.0), -1, keepdims=True)
     lane = lax.broadcasted_iota(jnp.int32, (8, 128), 0)
     stat[me] = jnp.where(
         lane == 0, across(peak), jnp.where(lane == 1, across(total_exp), across(hit))
@@ -679,15 +686,23 @@
     table = jnp.concatenate([logprob[:, c * n : (c + 1) * n] for c in range(choices)], 0)
     position = lax.broadcasted_iota(jnp.int32, table.shape, 1)
     choice = lax.broadcasted_iota(jnp.int32, table.shape, 0)
-    out_ref[...] = jnp.sum(jnp.where(position == me, table, 0.0), -1, keepdims=True)
+    own = jnp.sum(jnp.where(position == me, table, 0.0), -1, keepdims=True)
     length = jnp.zeros(table.shape, jnp.int32)
     for c in range(choices):
         length = jnp.where(choice == c, lengths_ref[c], length)
     usable = jnp.where((mask_ref[...] == 1) & (position < length), 1.0, 0.0)
     counted = jnp.maximum(jnp.sum(usable, -1, keepdims=True), 1.0)
     means = jnp.sum(table * usable, -1, keepdims=True) / counted
-    for c in range(choices):
-        scores_ref[c] = jnp.sum(means[c : c + 1])
+    diagonal = lax.broadcasted_iota(jnp.int32, (choices, 128), 0) == lax.broadcasted_iota(
+        jnp.int32, (choices, 128), 1
+    )
+
+    def flat(column):
+        wide = jnp.broadcast_to(column, (choices, 128))
+        return jnp.sum(jnp.where(diagonal, wide, 0.0), 0, keepdims=True)
+
+    first = lax.broadcasted_iota(jnp.int32, (8, 128), 0) == 0
+    out_ref[...] = jnp.where(first, flat(own), flat(means))
 
     @pl.loop(1, half)
     def _(d):
@@ -749,14 +764,11 @@
     sems = pltpu.SemaphoreType.DMA
     smem = pl.BlockSpec(memory_space=pltpu.SMEM)
     message = pltpu.VMEM((n, per_msg, HEAD_SIZE), BF16)
-    logprobs, scores = pl.pallas_call(
+    packed = pl.pallas_call(
         functools.partial(fused_kernel, n),
-        out_shape=(
-            jax.ShapeDtypeStruct((CHOICE_COUNT, 1), F32),
-            jax.ShapeDtypeStruct((CHOICE_COUNT,), F32),
-        ),
+        out_shape=jax.ShapeDtypeStruct((8, 128), F32),
         in_specs=[vmem] * 9 + [smem] + [hbm] * 2,
-        out_specs=(vmem, smem),
+        out_specs=vmem,
         scratch_shapes=[
             pltpu.VMEM((SLOTS, width, vocab), BF16),
             message,
@@ -793,20 +805,17 @@
             collective_id=0, has_side_effects=True, vmem_limit_bytes=67043328
         ),
     )(
-        queries,
-        residual,
-        answer_keys,
-        answer_values,
+        *(part.transpose(1, 0, 2)[0] for part in (queries, residual, answer_keys, answer_values)),
         cached_prefix_keys,
         cached_prefix_values,
         norm_gain.reshape(1, D),
-        targets.reshape(rows, 1),
+        targets,
         score_mask,
         lengths,
         out_weight,
         head_weight,
     )
-    return logprobs, scores
+    return packed[:1, :CHOICE_COUNT].T, packed[1, :CHOICE_COUNT]
 
 
 def either(*arrays):

time: 75.3 us -> 66.7 us (0.89)
  local copies, waits for them, and re-layouts: 9.56 us -> 1.26 us
    unnamed x5 -> x0, local copies, waits for them, and re-layouts: 6.92 us -> none
    reshape x1 -> x0, local copies, waits for them, and re-layouts: 1.37 us -> none  [fused(): targets.reshape(rows, 1)]
    pallas_call x1 -> x0, local copies, waits for them, and re-layouts: 1.27 us -> none  [fused(): pl.pallas_call(functools.partial(fused_kernel, n), out_shape=(jax.ShapeDt...]
    squeeze x0 -> x1, local copies, waits for them, and re-layouts: none -> 1.26 us  [fused(): return (packed[:1, :CHOICE_COUNT].T, packed[1, :CHOICE_COUNT])]
where the time goes in v1:
time: 66.7 us; the launch traced here: 66.5 us
  Pallas kernels  64.6 us (97%)
  local copies, waits for them, and re-layouts  1.26 us (2%)
    pallas_call x1, Pallas kernels, fused(): pl.pallas_call(functools.partial(fused_kernel, n), out_shape=jax.ShapeDty...  64.6 us

profile of v1, /device:TPU:0, one launch (start us, length us, event | category | flops | bytes accessed | tf_op | source)
XLA Modules:
  0.0 66.5 jit_solution(9116438895868638505)
XLA Ops:
  0.6 64.6 %shard_map.131 = f32[8,128]{1,0:T(8,128)} custom-call(bf16[4,8192]{1,0:T(4,128)(2,1)} %bitcast.9, bf16[4,8192]{1,0:T(4,128)(2,1)} %bitcast.10, bf16[4,1024]{1,0:T(4,128)(2,1)} %bitcast.12, bf16[4,1024]{1,0:T(4,128)(2,1)} %bitcast.13, bf16[64,1024]{1,0:T(8,128)(2,1)} %pk_ref.1, bf16[64,1024]{1,0:T(8,128)(2,1)} %pv_ref.1, f32[1,8192]{1,0:T(1,128)} %bitcast.11, ...), custom_call_target="tpu_custom_call" | custom-call | tf_op jit(solution)/shard_map/pallas_call | solution.py:767
  65.2 1.3 %slice_bitcast_fusion = (f32[4]{0:T(128)}, f32[4,1]{0,1:T(1,128)}) fusion(f32[8,128]{1,0:T(8,128)} %shard_map.131), kind=kLoop, calls=%fused_computation | loop fusion | bytes 64 | tf_op jit(solution)/shard_map/squeeze | solution.py:818
